TPU v7x, 32 devices: a whole 2x2x4 slice. The times are simulated.
32 devices in a mesh: row: 4 (over y, core), col: 8 (over z, x).
Axes of the slice: x: 2, y: 2, z: 4, core: 2. Of those that a mesh axis runs over, the one named last changes fastest.
Arguments:
- values: bfloat16 [8192, 128], P('row'), may hold values from -30 to 30
- points0: bfloat16 [2, 8192], P(None, 'row'), may hold values from 0 to 1
- points1: bfloat16 [2, 2048], P(None, 'row'), may hold values from 0 to 1
- points2: bfloat16 [2, 256], P(None, 'row'), may hold values from 0 to 1
- tiles_a0: int32 [4, 8, 2, 48], P('row', 'col'), may hold values from 0 to 15, as said below
- tiles_e1: int32 [4, 8, 2, 20], P('row', 'col'), may hold values from 0 to 15, as said below
- tiles_a1: int32 [4, 8, 2, 4], P('row', 'col'), may hold values from 0 to 3, as said below
- factor: bfloat16 [256, 256], P('row', 'col'), as said below
Outputs:
- fine_coef: float32 [8192, 128], P(('row', 'col'))
- mid_coef: float32 [2048, 128], P('col')
- coarse_coef: float32 [256, 128], P('row')
- norms: float32 [1], replicated
Inputs may be any that keep to these rules, and one draw needn't show every extreme that they name: `tiles_a0`: within each block the 48 listed tile pairs are distinct; tile rows are below 16 and tile columns below 8. `tiles_e1`: within each block the 20 listed tile pairs are distinct; tile rows are below 16 and tile columns below 2. `tiles_a1`: within each block the 4 listed tile pairs are distinct; tile rows are below 4 and tile columns below 2. `factor`: upper triangular; diagonal entries from 1 to 2.
All inputs are finite; a program needn't handle non-finite values.
Results may differ from a plain program's by a relative error of at most 0.0042.
Values may be sent and summed in bfloat16 or wider, within the bound.
A program may use at most 64 MiB of HBM per device.

v0:
```python
import math

import jax
import jax.numpy as jnp
from jax import lax
from jax.sharding import PartitionSpec as P

TILE = 128


support_fine = 0.35
support_mid = 0.55
support_coarse = 0.8


def spread(x, axis, root):
    mine = lax.axis_index(axis) == root
    return lax.psum(jnp.where(mine, x, jnp.zeros_like(x)), axis)


def wendland(left_pts, right_pts, support):
    left = left_pts.astype(jnp.float32)
    right = right_pts.astype(jnp.float32)
    across = left[0][..., :, None] - right[0][..., None, :]
    upward = left[1][..., :, None] - right[1][..., None, :]
    ratio_t = jnp.sqrt(across * across + upward * upward) / support
    margin = jnp.maximum(1.0 - ratio_t, 0.0)
    squared = margin * margin
    return (squared * squared * (4.0 * ratio_t + 1.0)).astype(jnp.bfloat16)


def listed_terms(row_pts, col_pts, listing, vector, support, flipped):
    row_tiles = row_pts.reshape(2, -1, TILE)
    col_tiles = col_pts.reshape(2, -1, TILE)
    listed = listing.shape[-1]
    group = math.gcd(listed, 32)
    order = listing.reshape(2, listed // group, group)
    fields = vector.shape[-1]
    inputs = vector.reshape(-1, TILE, fields)
    target = col_tiles.shape[1] if flipped else row_tiles.shape[1]
    total = jnp.zeros((target, TILE, fields), jnp.float32)

    def add_group(total, pair):
        tile_rows, tile_cols = pair
        kernel = wendland(row_tiles[:, tile_rows], col_tiles[:, tile_cols], support)
        if flipped:
            contrib = jnp.einsum(
                "gij,gir->gjr", kernel, inputs[tile_rows], preferred_element_type=jnp.float32
            )
            return (total.at[tile_cols].add(contrib), None)
        contrib = jnp.einsum(
            "gij,gjr->gir", kernel, inputs[tile_cols], preferred_element_type=jnp.float32
        )
        return (total.at[tile_rows].add(contrib), None)

    total, unused = lax.scan(add_group, total, (order[0], order[1]))
    return total.reshape(-1, fields)


def per_device(values, points0, points1, points2, tiles_a0, tiles_e1, tiles_a1, factor):
    row_count = lax.axis_size("row")
    col_count = lax.axis_size("col")
    col_id = lax.axis_index("col")
    col_per_row = col_count // row_count
    rows_fine, fields = values.shape
    rows_mid = points1.shape[1]
    share = rows_fine // col_count
    cols_fine = rows_fine // col_per_row
    cols_mid = rows_mid // col_per_row
    source = col_id // col_per_row
    part_index = col_id % col_per_row
    value_piece = lax.dynamic_slice_in_dim(values, part_index * cols_fine, cols_fine, 0)
    fine_piece = lax.dynamic_slice_in_dim(points0, part_index * cols_fine, cols_fine, 1)
    mid_piece = lax.dynamic_slice_in_dim(points1, part_index * cols_mid, cols_mid, 1)
    value_cols, fine_cols, mid_cols = (
        spread(value_piece, "row", source),
        spread(fine_piece, "row", source),
        spread(mid_piece, "row", source),
    )
    scale_a0 = (rows_fine / (col_count * tiles_a0.shape[-1] * TILE * TILE)) ** 0.5
    scale_e1 = (rows_fine / (col_count * tiles_e1.shape[-1] * TILE * TILE)) ** 0.5
    scale_a1 = (rows_mid / (col_count * tiles_a1.shape[-1] * TILE * TILE)) ** 0.5
    scale_e2 = (1.0 / (rows_mid * row_count)) ** 0.5
    fine_data = values.astype(jnp.float32)
    own_data = lax.dynamic_slice_in_dim(values, col_id * share, share, 0).astype(jnp.float32)
    product_part = listed_terms(points0, fine_cols, tiles_a0[0, 0], value_cols, support_fine, False)
    product_whole = lax.psum(product_part, "col")
    fine_residual = fine_data - 0.5 * (scale_a0 * product_whole)
    fine_square = jnp.sum(fine_residual * fine_residual)
    restrict_part = listed_terms(
        points0, mid_cols, tiles_e1[0, 0], fine_residual.astype(jnp.bfloat16), support_mid, True
    )
    restrict_sum = lax.psum(restrict_part, "row")
    mid_data = scale_e1 * restrict_sum
    mid_part = listed_terms(
        points1, mid_cols, tiles_a1[0, 0], mid_data.astype(jnp.bfloat16), support_mid, False
    )
    mid_whole = (scale_a1 * lax.psum(mid_part, "col")).astype(jnp.bfloat16)
    mid_slice = lax.dynamic_slice_in_dim(mid_whole, part_index * cols_mid, cols_mid, 0)
    mid_turned = spread(mid_slice, "row", source)
    mid_residual = mid_data - 0.5 * mid_turned.astype(jnp.float32)
    coarse_kernel = wendland(points2, mid_cols, support_coarse)
    coarse_part = jnp.dot(
        coarse_kernel, mid_residual.astype(jnp.bfloat16), preferred_element_type=jnp.float32
    )
    coarse_sum = lax.psum(coarse_part, "col")
    coarse_data = (scale_e2 * coarse_sum).astype(jnp.bfloat16)
    halfway_part = lax.dot_general(
        factor, coarse_data, (((0,), (0,)), ((), ())), preferred_element_type=jnp.float32
    )
    halfway = lax.psum(halfway_part, "row").astype(jnp.bfloat16)
    coarse_part_two = jnp.dot(factor, halfway, preferred_element_type=jnp.float32)
    coarse_coef = lax.psum(coarse_part_two, "col")
    prolong_part = lax.dot_general(
        coarse_kernel,
        coarse_coef.astype(jnp.bfloat16),
        (((0,), (0,)), ((), ())),
        preferred_element_type=jnp.float32,
    )
    mid_coef = 0.5 * mid_data + scale_e2 * lax.psum(prolong_part, "row")
    fine_part = listed_terms(
        points0, mid_cols, tiles_e1[0, 0], mid_coef.astype(jnp.bfloat16), support_mid, False
    )
    fine_coef = 0.5 * own_data + scale_e1 * lax.psum_scatter(
        fine_part, "col", scatter_dimension=0, tiled=True
    )
    fine_total = lax.psum(fine_square / col_count, ("row", "col"))
    fine_norm = fine_total / (rows_fine * row_count * fields)
    return (fine_coef, mid_coef, coarse_coef, jnp.stack([fine_norm]))


def solution(mesh):
    return jax.shard_map(
        per_device,
        mesh=mesh,
        in_specs=(
            P("row", None),
            P(None, "row"),
            P(None, "row"),
            P(None, "row"),
            P("row", "col", None, None),
            P("row", "col", None, None),
            P("row", "col", None, None),
            P("row", "col"),
        ),
        out_specs=(P(("row", "col"), None), P("col", None), P("row", None), P()),
        check_vma=False,
    )
```

profile of v0, /device:TPU:0, one launch (start us, length us, event | category | flops | bytes accessed | tf_op | source)
XLA Modules:
  0.0 501.4 jit_solution(3732552858694689181)
XLA Ops:
  7.3 1.7 dynamic-slice_select_fusion
  9.1 0.7 copy-done.11
  9.7 0.7 copy-done.12
  10.4 0.7 copy-done.10
  11.9 8.5 %all-reduce = (bf16[2,256]{1,0:T(2,128)(2,1)S(1)}, bf16[2,8,128]{2,0,1:T(2,128)(2,1)S(1)}) all-reduce(bf16[2,256]{1,0:T(2,128)(2,1)S(1)} %broadcast_select_fusion.1, bf16[2,8,128]{2,0,1:T(2,128)(2,1)S(1)} %fusion.64), channel_id=1, replica_groups=mesh['row'=4,'col'=8] {'row'}, use_global_device_ids=true, to_apply=%region_0.1 | all-reduce | flops 2560 | bytes 10240 | tf_op jit(solution)/shard_map/psum | solution.py:18
  20.4 24.9 %all-reduce.8.cloned.1.call-done = bf16[8,128,128]{2,1,0:T(8,128)(2,1)} async-done(((bf16[8,128,128]{2,1,0:T(8,128)(2,1)}), bf16[8,128,128]{2,1,0:T(8,128)(2,1)}) %all-reduce.8.cloned.1.call-update) | async-done | bytes 262160 | tf_op jit(solution)/shard_map/psum | solution.py:18
  45.5 0.8 copy-done.2
  46.3 15.2 %while.40 = (s32[]{:T(128)}, f32[16,128,128]{2,1,0:T(8,128)S(1)}, s32[3,16]{1,0:T(4,128)S(1)}, bf16[2,16,128]{2,0,1:T(2,128)(2,1)S(1)}, s32[3,16]{1,0:T(4,128)S(...) while((s32[]{:T(128)}, f32[16,128,128]{2,1,0:T(8,128)S(1)}, ...), condition=%wide.region_5.6_spmd, body=%wide.region_3.5_spmd.sunk | while | flops 71051360 | bytes 5956313 | solution.py:56
  46.3 0.6 gather_fusion.1
  47.0 0.6 gather_fusion.2
  47.6 0.6 gather_fusion
  48.2 1.5 fusion.118
  49.7 1.6 scatter_fusion
  51.4 0.6 gather_fusion.1
  52.0 0.6 gather_fusion.2
  52.7 0.6 gather_fusion
  53.3 1.5 fusion.118
  54.8 1.6 scatter_fusion
  56.5 0.6 gather_fusion.1
  57.1 0.6 gather_fusion.2
  57.7 0.6 gather_fusion
  58.4 1.5 fusion.118
  59.9 1.6 scatter_fusion
  61.6 1.0 copy-done.1
  62.7 0.6 gather_fusion.10
  63.3 0.6 gather_fusion.9
  63.9 77.0 %all-reduce.10.cloned.1.call-done = f32[2048,128]{1,0:T(8,128)} async-done(((f32[2048,128]{1,0:T(8,128)}), f32[2048,128]{1,0:T(8,128)}) %all-reduce.10.cloned.1.call-update) | async-done | bytes 1048592 | tf_op jit(solution)/shard_map/psum | solution.py:87
  140.9 2.2 multiply_reduce_fusion
  143.1 14.8 %while.41 = (s32[]{:T(128)}, f32[2,128,128]{2,1,0:T(8,128)S(1)}, s32[5,4]{1,0:T(8,128)S(1)}, s32[5,4]{1,0:T(8,128)S(1)}, bf16[2,16,128]{2,0,1:T(2,128)(2,1)S(1)}...) while((s32[]{:T(128)}, f32[2,128,128]{2,1,0:T(8,128)S(1)}, ...), condition=%wide.region_9.10_spmd, body=%wide.region_7.9_spmd.sunk | while | flops 17764376 | bytes 1495289 | solution.py:56
  143.1 0.6 gather_fusion.4
  143.7 0.6 gather_fusion.5
  145.3 0.8 scatter_fusion.1
  146.1 0.6 gather_fusion.4
  146.7 0.6 gather_fusion.5
  148.2 0.7 scatter_fusion.1
  149.0 0.6 gather_fusion.4
  151.2 0.8 scatter_fusion.1
  154.1 0.8 scatter_fusion.1
  157.1 0.8 scatter_fusion.1
  157.9 0.6 copy-done.3
  158.6 31.5 %all-reduce.12.cloned.1.call-done = f32[256,128]{1,0:T(8,128)} async-done(((f32[256,128]{1,0:T(8,128)}), f32[256,128]{1,0:T(8,128)}) %all-reduce.12.cloned.1.call-update) | async-done | bytes 131088 | tf_op jit(solution)/shard_map/psum | solution.py:93
  190.1 0.9 multiply_convert_fusion.8
  192.0 0.7 scatter_fusion.3
  192.8 0.7 copy-done.5
  193.6 71.1 %all-reduce.14.cloned.1.call-done = f32[512,128]{1,0:T(8,128)} async-done(((f32[512,128]{1,0:T(8,128)}), f32[512,128]{1,0:T(8,128)}) %all-reduce.14.cloned.1.call-update) | async-done | bytes 262160 | tf_op jit(solution)/shard_map/psum | solution.py:98
  264.6 1.6 fusion.57
  266.3 31.9 %all-reduce.16.cloned.1.call-done = bf16[256,128]{1,0:T(8,128)(2,1)} async-done(((bf16[256,128]{1,0:T(8,128)(2,1)}), bf16[256,128]{1,0:T(8,128)(2,1)}) %all-reduce.16.cloned.1.call-update) | async-done | bytes 65552 | tf_op jit(solution)/shard_map/psum | solution.py:18
  298.1 1.1 fusion.56
  299.2 37.1 %psum.91 = f32[64,128]{1,0:T(8,128)S(1)} all-reduce(f32[64,128]{1,0:T(8,128)S(1)} %fusion.56), channel_id=1, replica_groups=mesh['row'=4,'col'=8] {'col'}, use_global_device_ids=true, to_apply=%region_14.15 | all-reduce | flops 8192 | bytes 65536 | tf_op jit(solution)/shard_map/psum | solution.py:106
  336.5 10.8 %psum.92 = bf16[32,128]{0,1:T(8,128)(2,1)S(1)} all-reduce(f32[32,128]{0,1:T(8,128)S(1)} %convolution_bitcast_fusion), channel_id=1, replica_groups=mesh['row'=4,'col'=8] {'row'}, use_global_device_ids=true, to_apply=%region_15.16 | all-reduce | flops 4096 | bytes 24576 | tf_op jit(solution)/shard_map/psum | solution.py:111
  347.5 33.0 %psum.93 = f32[64,128]{1,0:T(8,128)S(1)} all-reduce(f32[64,128]{1,0:T(8,128)S(1)} %convolution_bitcast_fusion.1), channel_id=1, replica_groups=mesh['row'=4,'col'=8] {'col'}, use_global_device_ids=true, to_apply=%region_16.17 | all-reduce | flops 8192 | bytes 65536 | tf_op jit(solution)/shard_map/psum | solution.py:113
  380.5 1.0 fusion.61
  381.6 28.0 %all-reduce.18.cloned.1.call-done = f32[256,128]{1,0:T(8,128)} async-done(((f32[256,128]{1,0:T(8,128)}), f32[256,128]{1,0:T(8,128)}) %all-reduce.18.cloned.1.call-update) | async-done | bytes 131088 | tf_op jit(solution)/shard_map/psum | solution.py:120
  409.5 1.6 fusion.82
  411.2 14.8 %while.42 = (s32[]{:T(128)}, f32[16,128,128]{2,1,0:T(8,128)S(1)}, s32[5,4]{1,0:T(8,128)S(1)}, bf16[2,16,128]{2,0,1:T(2,128)(2,1)S(1)}, s32[5,4]{1,0:T(8,128)S(1)...) while((s32[]{:T(128)}, f32[16,128,128]{2,1,0:T(8,128)S(1)}, ...), condition=%wide.region_20.21_spmd, body=%wide.region_18.20_spmd.sunk | while | flops 17764376 | bytes 1495289 | solution.py:56
  413.4 0.8 scatter_fusion.2
  416.4 0.8 scatter_fusion.2
  419.3 0.8 scatter_fusion.2
  422.3 0.8 scatter_fusion.2
  425.2 0.8 scatter_fusion.2
  426.0 1.0 copy-done.4
  427.7 39.4 %psum.95 = f32[]{:T(128)} all-reduce(f32[]{:T(128)S(6)} %div.39), channel_id=1, replica_groups=mesh['row'=4,'col'=8] {'row','col'}, use_global_device_ids=true, to_apply=%region_23.24 | all-reduce | flops 1 | bytes 8 | tf_op jit(solution)/shard_map/psum | solution.py:127
  467.7 24.1 %reduce-scatter.2.cloned.1.call-done = f32[256,128]{1,0:T(8,128)} async-done(((f32[2048,128]{1,0:T(8,128)}), f32[256,128]{1,0:T(8,128)}) %reduce-scatter.2.cloned.1.call-update) | async-done | bytes 131088 | tf_op jit(solution)/shard_map/reduce_scatter | solution.py:124
  491.8 1.6 multiply_add_fusion
  (188 shorter events, 21.6 us)
Async XLA Ops:
  7.2 329.1 %copy-start = (bf16[64,32]{0,1:T(8,128)(2,1)S(1)}, bf16[64,32]{0,1:T(8,128)(2,1)}, u32[]{:S(2)}) copy-start(bf16[64,32]{0,1:T(8,128)(2,1)} %param.21) | copy-start | bytes 12292
  7.2 38.2 %all-reduce.8.cloned.1.call-start = ((), (), s32[]{:S(2)}) async-start(), calls=%async_computation.1 | async-start | bytes 524288 | tf_op jit(solution)/shard_map/psum | solution.py:18
  9.0 131.9 %all-reduce.10.cloned.1.call-start = ((), (), s32[]{:S(2)}) async-start(), calls=%async_computation.2 | async-start | bytes 2097152 | tf_op jit(solution)/shard_map/psum | solution.py:87
  9.0 0.7 copy-start.11
  9.7 0.7 copy-start.12
  10.4 0.7 copy-start.10
  11.2 0.7 copy-start.8
  45.4 0.9 copy-start.2
  61.5 1.0 copy-start.1
  61.5 1.1 copy-start.13
  61.6 79.3 %copy-start.6 = (bf16[2048,128]{1,0:T(8,128)(2,1)S(1)}, bf16[2048,128]{1,0:T(8,128)(2,1)}, u32[]{:S(2)}) copy-start(bf16[2048,128]{1,0:T(8,128)(2,1)} %param.14) | copy-start | bytes 1572868
  62.6 127.5 %all-reduce.12.cloned.1.call-start = ((), (), s32[]{:S(2)}) async-start(), calls=%async_computation.3 | async-start | bytes 262144 | tf_op jit(solution)/shard_map/psum | solution.py:93
  157.8 0.7 copy-start.3
  158.5 106.1 %all-reduce.14.cloned.1.call-start = ((), (), s32[]{:S(2)}) async-start(), calls=%async_computation.4 | async-start | bytes 524288 | tf_op jit(solution)/shard_map/psum | solution.py:98
  192.7 0.7 copy-start.5
  192.7 0.8 copy-start.14
  193.5 104.7 %all-reduce.16.cloned.1.call-start = ((), (), s32[]{:S(2)}) async-start(), calls=%async_computation.5 | async-start | bytes 131072 | tf_op jit(solution)/shard_map/psum | solution.py:18
  193.5 104.6 %copy-start.7 = (f32[256,128]{1,0:T(8,128)S(1)}, f32[256,128]{1,0:T(8,128)}, u32[]{:S(2)}) copy-start(f32[256,128]{1,0:T(8,128)} %all-reduce.12.cloned.1.call-done) | copy-start | bytes 393220
  266.2 143.3 %all-reduce.18.cloned.1.call-start = ((), (), s32[]{:S(2)}) async-start(), calls=%async_computation.6 | async-start | bytes 262144 | tf_op jit(solution)/shard_map/psum | solution.py:120
  380.5 1.0 copy-start.9
  381.5 110.3 %reduce-scatter.2.cloned.1.call-start = ((), (), s32[]{:S(2)}) async-start(), calls=%async_computation.7 | async-start | bytes 1179648 | tf_op jit(solution)/shard_map/reduce_scatter | solution.py:124
  426.0 1.0 copy-start.4
Sparse Core Ops, SparseCore 0:
  10.3 34.9 all-reduce.7
  62.7 78.1 all-reduce.9
  158.6 31.3 all-reduce.11
  193.6 70.9 all-reduce.13
  267.4 30.7 all-reduce.15
  381.6 27.8 all-reduce.17
  427.2 64.5 reduce-scatter.1
where the time goes:
time: 502 us; the launch traced here: 501 us
  waiting for transfers between devices  289 us (58%)
  blocking collectives  129 us (26%)
  local copies, waits for them, and re-layouts  31.9 us (6%)
  other arithmetic  23.1 us (5%)
  between operations  16.8 us (3%)
  matrix products  10.9 us (2%)
    psum x1, waiting for transfers between devices, per_device(): product_whole = lax.psum(product_part, 'col')  77 us
    psum x1, waiting for transfers between devices, per_device(): mid_whole = (scale_a1 * lax.psum(mid_part, 'col')).astype(jnp.bfloat16)  71.1 us
    psum x2, waiting for transfers between devices, spread(): return lax.psum(jnp.where(mine, x, jnp.zeros_like(x)), axis)  56.8 us
    psum x1, blocking collectives, per_device(): fine_total = lax.psum(fine_square / col_count, ('row', 'col'))  39.4 us
    psum x1, blocking collectives, per_device(): coarse_sum = lax.psum(coarse_part, 'col')  37.1 us
    psum x1, blocking collectives, per_device(): coarse_coef = lax.psum(coarse_part_two, 'col')  33 us
    psum x1, waiting for transfers between devices, per_device(): restrict_sum = lax.psum(restrict_part, 'row')  31.5 us
    psum x1, waiting for transfers between devices, per_device(): mid_coef = 0.5 * mid_data + scale_e2 * lax.psum(prolong_part, 'row')  28 us
  transfers between devices with their start and end apart: 7, of which 7 were waited for; matrix products, arithmetic and copies ran while one was open for 0% of the time, Pallas kernels for 0%

commit v1 on v0

--- a/solution.py
+++ b/solution.py
@@ -1,8 +1,11 @@
+import functools
 import math
 
 import jax
 import jax.numpy as jnp
 from jax import lax
+from jax.experimental import pallas as pl
+from jax.experimental.pallas import tpu as pltpu
 from jax.sharding import PartitionSpec as P
 
 TILE = 128
@@ -129,9 +132,396 @@
     return (fine_coef, mid_coef, coarse_coef, jnp.stack([fine_norm]))
 
 
+FAR = 1024.0
+CHUNKS = 4
+MESH = pl.DeviceIdType.MESH
+
+
+def phi_tile(cx, cy, rx, ry, inv_square):
+    across = cx - rx
+    upward = cy - ry
+    square = (across * across + upward * upward) * inv_square
+    t = square * lax.rsqrt(jnp.maximum(square, 1e-30))
+    margin = jnp.maximum(1.0 - t, 0.0)
+    squared = margin * margin
+    return (squared * squared * (4.0 * t + 1.0)).astype(jnp.bfloat16)
+
+
+def dot(a, b):
+    return jnp.dot(a, b, preferred_element_type=jnp.float32)
+
+
+def cycle_kernel(g, vals, pts, offs, fac, offe, offa, fine_o, mid_o, coarse_o, norm_o,
+                 ptsg, offg, facg, vall, a0, e1own, e1t, e2t, e2c, a1, cf, cm, cc2, resg, part_buf,
+                 rsin, midc, mida, rhs, csend, crecv, cg, gall, gt, ccoef, mcb,
+                 p_s, p_r, o_s, o_r, f_s, f_r, vy_s, vy_r, vx_s, vx_r, vf_s, vf_r, vg_s, vg_r, vp_s, vp_r,
+                 g_s, g_r, res_s, res_r, rs_s, rs_r, mc_s, mc_r, mq_s, mq_r, mf_s, mf_r, cr_s, cr_r, ca_s, ca_r):
+    nr, nc, R0, R1, R2 = g["nr"], g["nc"], g["R0"], g["R1"], g["R2"]
+    D = nr * nc
+    T0, T1 = R0 // TILE, R1 // TILE
+    C0, C1 = R0 * nr // nc, R1 * nr // nc
+    B0, B1 = C0 // TILE, C1 // TILE
+    S0 = R0 // nc
+    I0 = S0 // TILE
+    Q1 = C1 // nr
+    CR = R2 * nr // D
+    NT1 = nr * T1
+    NT2 = nr * R2 // TILE
+    X1, Y1, X2 = 2 * T0, 2 * T0 + T1, 2 * T0 + 2 * T1
+    fine_inv, mid_inv, coarse_inv = (1.0 / (s * s) for s in (support_fine, support_mid, support_coarse))
+    r = lax.axis_index("row")
+    c = lax.axis_index("col")
+    d = r * nc + c
+    mate = r + 1 - 2 * lax.rem(r, 2)
+    yp = lax.rem(r + 2, nr)
+    diag = lax.rem(mate + 2, nr)
+    h = lax.rem(c, 2)
+    xp = c + 1 - 2 * h
+
+    def rc(src, dst, ssem, rsem, rr, cc):
+        return pltpu.make_async_remote_copy(src_ref=src, dst_ref=dst, send_sem=ssem, recv_sem=rsem,
+                                            device_id=(rr, cc), device_id_type=MESH)
+
+    def each(lo, hi, f):
+        def body(k, carry):
+            f(k)
+            return carry
+        lax.fori_loop(lo, hi, body, 0)
+
+    barrier = pltpu.get_barrier_semaphore()
+
+    def greet(k):
+        peer = lax.rem(d + k, D)
+        pl.semaphore_signal(barrier, inc=1, device_id=(peer // nc, lax.rem(peer, nc)), device_id_type=MESH)
+
+    each(1, D, greet)
+    pl.semaphore_wait(barrier, D - 1)
+
+    def row_send(src_of, dst, ss, rr):
+        for k in range(1, nr):
+            q = lax.rem(r + k, nr)
+            rc(src_of(q), dst, ss.at[k], rr.at[r], q, c).start()
+
+    def row_wait(src, dst_of, ss, rr):
+        for k in range(1, nr):
+            q = lax.rem(r + k, nr)
+            rc(src, dst_of(q), ss.at[k], rr.at[q], q, c).wait()
+
+    def col_send(src_of, dst, ss, rr):
+        def go(k):
+            q = lax.rem(c + k, nc)
+            rc(src_of(q), dst, ss.at[k], rr.at[c], r, q).start()
+        each(1, nc, go)
+
+    def col_wait(src, dst_of, ss, rr):
+        def go(k):
+            q = lax.rem(c + k, nc)
+            rc(src, dst_of(q), ss.at[k], rr.at[q], r, q).wait()
+        each(1, nc, go)
+
+    row_send(lambda q: pts, ptsg.at[r], p_s, p_r)
+    HALF = R0 // 2
+    CH = HALF // CHUNKS
+
+    def chunk(half, q):
+        return pl.ds(pl.multiple_of(half * HALF + q * CH, CH), CH)
+
+    def y_copy(q):
+        return rc(vals.at[chunk(h, q)], vall.at[r, chunk(h, q)], vy_s.at[q], vy_r.at[q], yp, c)
+
+    def y_in(q):
+        return rc(vals.at[chunk(h, q)], vall.at[yp, chunk(h, q)], vy_s.at[q], vy_r.at[q], yp, c)
+
+    def x_copy(q):
+        return rc(vall.at[yp, chunk(h, q)], vall.at[yp, chunk(h, q)], vx_s.at[q], vx_r.at[q], r, xp)
+
+    def x_in(q):
+        return rc(vall.at[yp, chunk(h, q)], vall.at[yp, chunk(1 - h, q)], vx_s.at[q], vx_r.at[q], r, xp)
+
+    def f_copy(q):
+        return rc(vall.at[yp, chunk(h, q)], vall.at[yp, chunk(h, q)], vf_s.at[q], vf_r.at[q], mate, c)
+
+    def f_in(q):
+        return rc(vall.at[yp, chunk(h, q)], vall.at[diag, chunk(h, q)], vf_s.at[q], vf_r.at[q], mate, c)
+
+    def g_copy(q):
+        return rc(vall.at[yp, chunk(1 - h, q)], vall.at[yp, chunk(1 - h, q)], vg_s.at[q], vg_r.at[q], mate, c)
+
+    def g_in(q):
+        return rc(vall.at[yp, chunk(1 - h, q)], vall.at[diag, chunk(1 - h, q)], vg_s.at[q], vg_r.at[q], mate, c)
+
+    for q in range(CHUNKS):
+        y_copy(q).start()
+    col_send(lambda q: offs.at[q], offg.at[c], o_s, o_r)
+    mate_copy = rc(vals, vall.at[r], vp_s.at[0], vp_r.at[0], mate, c)
+    mate_copy.start()
+    col_send(lambda q: fac, facg.at[c], f_s, f_r)
+    ptsg[r] = pts[...]
+    offg[c] = offs[c]
+    facg[c] = fac[...]
+
+    def turned(row):
+        return jnp.broadcast_to(row, (TILE, TILE)).T
+
+    for i in range(I0):
+        for way in range(2):
+            cf[2 * i + way] = turned(pts[pl.ds(way * T0 + c * I0 + i, 1), :])
+    row_wait(pts, lambda q: ptsg.at[q], p_s, p_r)
+    col_wait(offs.at[0], lambda q: offg.at[q], o_s, o_r)
+
+    blocks = (r, mate, yp, diag)
+    for s, rb in enumerate(blocks):
+        def build_a0(kk, s=s, rb=rb):
+            rx = ptsg[rb, pl.ds(kk, 1), :]
+            ry = ptsg[rb, pl.ds(T0 + kk, 1), :]
+            cb = rb * (nc // nr) + kk // B0
+            j = lax.rem(kk, B0)
+            for i in range(I0):
+                off = offg[cb, pl.ds(i * B0 + j, 1), :]
+                a0[s, i * TILE:(i + 1) * TILE, pl.ds(pl.multiple_of(kk * TILE, TILE), TILE)] = phi_tile(
+                    cf[2 * i], cf[2 * i + 1], rx + off, ry, fine_inv)
+        each(0, T0, build_a0)
+        if s < CHUNKS:
+            y_in(s).wait_recv()
+            x_copy(s).start()
+            f_copy(s).start()
+    acc = dot(a0[0], vals[...])
+    for q in range(CHUNKS):
+        x_in(q).wait_recv()
+        g_copy(q).start()
+    rc(vals, vall.at[mate], vp_s.at[0], vp_r.at[0], mate, c).wait_recv()
+    acc = acc + dot(a0[1], vall[mate])
+    acc = acc + dot(a0[2], vall[yp])
+    for q in range(CHUNKS):
+        f_in(q).wait_recv()
+        g_in(q).wait_recv()
+    acc = acc + dot(a0[3], vall[diag])
+    own_vals = vals[pl.ds(pl.multiple_of(c * S0, S0), S0), :].astype(jnp.float32)
+    res = own_vals - (0.5 * g["scale_a0"]) * acc
+    square = jnp.sum((res * res).reshape(S0 // 8, 8, -1), axis=0)
+
+    def res_at(q):
+        return resg.at[pl.ds(pl.multiple_of(q * S0, S0), S0)]
+
+    resg[pl.ds(pl.multiple_of(c * S0, S0), S0), :] = res.astype(jnp.bfloat16)
+    col_send(lambda q: res_at(c), res_at(c), res_s, res_r)
+
+    def turn_mid(k):
+        for way in range(2):
+            cm[k, way] = turned(ptsg[k // T1, pl.ds(X1 + way * T1 + lax.rem(k, T1), 1), :])
+    each(0, NT1, turn_mid)
+
+    def build_e1t(i):
+        rx, ry = pts[pl.ds(i, 1), :], pts[pl.ds(T0 + i, 1), :]
+        for j in range(B1):
+            off = offe[pl.ds(j * T0 + i, 1), :]
+            e1t[j * TILE:(j + 1) * TILE, pl.ds(pl.multiple_of(i * TILE, TILE), TILE)] = phi_tile(
+                cm[c * B1 + j, 0], cm[c * B1 + j, 1], rx + off, ry, mid_inv)
+    each(0, T0, build_e1t)
+    col_wait(fac, lambda q: facg.at[q], f_s, f_r)
+    per_lane = nc * TILE // g["N2"]
+    for lane in range(g["N2"] // TILE):
+        total = facg[lane * per_lane].astype(jnp.float32)
+        for k in range(1, per_lane):
+            total = total + facg[lane * per_lane + k].astype(jnp.float32)
+        gall[r, :, lane * TILE:(lane + 1) * TILE] = total.astype(jnp.bfloat16)
+    row_send(lambda q: gall.at[r], gall.at[r], g_s, g_r)
+
+    def coarse_row(t, way):
+        per = TILE // R2
+        return ptsg[per * t, X2 + way:X2 + way + 1, :] + ptsg[per * t + 1, X2 + 2 + way:X2 + 3 + way, :]
+
+    for i in range(T1):
+        for j in range(B1):
+            mt = c * B1 + j
+            rx = ptsg[mt // T1, pl.ds(X1 + lax.rem(mt, T1), 1), :]
+            ry = ptsg[mt // T1, pl.ds(Y1 + lax.rem(mt, T1), 1), :]
+            off = offa[i * B1 + j:i * B1 + j + 1, :]
+            a1[i * TILE:(i + 1) * TILE, j * TILE:(j + 1) * TILE] = phi_tile(
+                cm[r * T1 + i, 0], cm[r * T1 + i, 1], rx + off, ry, mid_inv)
+    for t in range(NT2):
+        for way in range(2):
+            cc2[2 * t + way] = turned(coarse_row(t, way))
+
+    def build_e2c(k):
+        mt = jnp.where(k < T1, r * T1 + k, c * B1 + k - T1)
+        rx = ptsg[mt // T1, pl.ds(X1 + lax.rem(mt, T1), 1), :]
+        ry = ptsg[mt // T1, pl.ds(Y1 + lax.rem(mt, T1), 1), :]
+        for t in range(NT2):
+            e2c[t * TILE:(t + 1) * TILE, pl.ds(pl.multiple_of(k * TILE, TILE), TILE)] = phi_tile(
+                cc2[2 * t], cc2[2 * t + 1], rx, ry, coarse_inv)
+    each(0, T1 + B1, build_e2c)
+
+    def build_e1own(k):
+        rx = ptsg[k // T1, pl.ds(X1 + lax.rem(k, T1), 1), :]
+        ry = ptsg[k // T1, pl.ds(Y1 + lax.rem(k, T1), 1), :]
+        for i in range(I0):
+            off = offg[k // B1, pl.ds(I0 * B0 + i * B1 + lax.rem(k, B1), 1), :]
+            e1own[i * TILE:(i + 1) * TILE, pl.ds(pl.multiple_of(k * TILE, TILE), TILE)] = phi_tile(
+                cf[2 * i], cf[2 * i + 1], rx + off, ry, mid_inv)
+    each(0, NT1, build_e1own)
+
+    def build_e2t(k):
+        for t in range(NT2):
+            e2t[pl.ds(pl.multiple_of(k * TILE, TILE), TILE), t * TILE:(t + 1) * TILE] = phi_tile(
+                cm[k, 0], cm[k, 1], coarse_row(t, 0), coarse_row(t, 1), coarse_inv)
+    each(0, NT1, build_e2t)
+    row_wait(gall.at[r], lambda q: gall.at[q], g_s, g_r)
+    whole = gall[...].reshape(g["N2"], g["N2"])
+    gt[...] = whole.astype(jnp.float32).T.astype(jnp.bfloat16)
+
+    col_wait(res_at(c), res_at, res_s, res_r)
+    part_buf[...] = dot(e1t[...], resg[...]).reshape(nr, Q1, -1)
+    row_send(lambda q: part_buf.at[q], rsin.at[r], rs_s, rs_r)
+    rsin[r] = part_buf[r]
+    row_wait(part_buf.at[0], lambda q: rsin.at[q], rs_s, rs_r)
+    quarter = rsin[0]
+    for k in range(1, nr):
+        quarter = quarter + rsin[k]
+    quarter = g["scale_e1"] * quarter
+    midc[r] = quarter
+    mida[r, c] = quarter.astype(jnp.bfloat16)
+    row_send(lambda q: midc.at[r], midc.at[r], mc_s, mc_r)
+    col_send(lambda q: mida.at[r, c], mida.at[r, c], mq_s, mq_r)
+    row_wait(midc.at[r], lambda q: midc.at[q], mc_s, mc_r)
+    mid_col = midc[...].reshape(C1, -1).astype(jnp.bfloat16)
+    rhs[:R1] = ((-0.5 * g["scale_a1"]) * dot(a1[...], mid_col)).astype(jnp.bfloat16)
+    for k in range(nr):
+        rhs[R1 + k * Q1:R1 + (k + 1) * Q1] = jnp.where(r == k, midc[k], 0.0).astype(jnp.bfloat16)
+    csend[:, :CR] = (g["scale_e2"] * dot(e2c[...], rhs[...])).reshape(D, CR, -1)
+    csend[:, CR:] = jnp.broadcast_to(square[None], (D,) + square.shape)
+
+    def cr_go(k):
+        peer = lax.rem(d + k, D)
+        rc(csend.at[peer], crecv.at[d], cr_s.at[k], cr_r.at[d], peer // nc, lax.rem(peer, nc)).start()
+    each(1, D, cr_go)
+    crecv[d] = csend[d]
+    col_wait(mida.at[r, c], lambda q: mida.at[r, q], mq_s, mq_r)
+    def cr_wait(k):
+        peer = lax.rem(d + k, D)
+        rc(csend.at[peer], crecv.at[peer], cr_s.at[k], cr_r.at[peer], peer // nc, lax.rem(peer, nc)).wait()
+    each(1, D, cr_wait)
+    sums = jnp.sum(crecv[...], axis=0)
+
+    def cg_at(q):
+        return cg.at[pl.ds(pl.multiple_of(q * CR, CR), CR)]
+
+    cg[pl.ds(pl.multiple_of(d * CR, CR), CR), :] = sums[:CR]
+
+    def ca_go(k):
+        peer = lax.rem(d + k, D)
+        rc(cg_at(d), cg_at(d), ca_s.at[k], ca_r.at[d], peer // nc, lax.rem(peer, nc)).start()
+    each(1, D, ca_go)
+    row_send(lambda q: mida.at[r], mida.at[r], mf_s, mf_r)
+    norm_o[...] = jnp.broadcast_to(jnp.sum(sums[CR:], keepdims=True) * g["norm_scale"], norm_o.shape)
+    def ca_wait(k):
+        peer = lax.rem(d + k, D)
+        rc(cg_at(d), cg_at(peer), ca_s.at[k], ca_r.at[peer], peer // nc, lax.rem(peer, nc)).wait()
+    each(1, D, ca_wait)
+    halfway = dot(gt[...], cg[...].astype(jnp.bfloat16)).astype(jnp.bfloat16)
+    ccoef[...] = dot(gall[...].reshape(g["N2"], g["N2"]), halfway)
+    coarse_o[...] = ccoef[pl.ds(pl.multiple_of(r * R2, R2), R2), :]
+    coarse_low = ccoef[...].astype(jnp.bfloat16)
+    own_rows = pl.ds(pl.multiple_of(c * C1, C1), C1)
+    mid_o[...] = 0.5 * midc[...].reshape(C1, -1) + g["scale_e2"] * dot(e2t[own_rows, :], coarse_low)
+    row_wait(mida.at[r], lambda q: mida.at[q], mf_s, mf_r)
+    for q in range(nc):
+        corr = g["scale_e2"] * dot(e2t[q * C1:(q + 1) * C1, :], coarse_low)
+        for k in range(nr):
+            mcb[q * C1 + k * Q1:q * C1 + (k + 1) * Q1] = (
+                0.5 * mida[k, q].astype(jnp.float32) + corr[k * Q1:(k + 1) * Q1]).astype(jnp.bfloat16)
+    fine_o[...] = 0.5 * own_vals + g["scale_e1"] * dot(e1own[...], mcb[...])
+    for q in range(CHUNKS):
+        y_copy(q).wait_send()
+        x_copy(q).wait_send()
+        f_copy(q).wait_send()
+        g_copy(q).wait_send()
+    mate_copy.wait_send()
+
+
+def far_of(listing, row_tiles, col_tiles):
+    key = listing[0] * col_tiles + listing[1]
+    hit = jnp.any(jnp.arange(row_tiles * col_tiles)[:, None] == key[None, :], axis=1)
+    return jnp.where(hit, 0.0, FAR).astype(jnp.float32).reshape(row_tiles, col_tiles)
+
+
+def fits(nr, nc, R0, R1, R2):
+    if nr != 4 or nc % nr or (nc // nr) % 2:
+        return False
+    if R0 % (nc * TILE) or (R1 * nr) % (nc * TILE) or R1 % TILE or 2 * R2 != TILE:
+        return False
+    if (nr * R2) % (nr * nc * 8) or (nr * R2) % TILE or (nc * TILE) % (nr * R2):
+        return False
+    return 2 * (R0 // nc) * R0 * nr <= 8 << 20
+
+
+def fused(values, points0, points1, points2, tiles_a0, tiles_e1, tiles_a1, factor):
+    nr, nc = lax.axis_size("row"), lax.axis_size("col")
+    R0, R1, R2 = points0.shape[1], points1.shape[1], points2.shape[1]
+    F = values.shape[-1]
+    if not fits(nr, nc, R0, R1, R2) or F != TILE:
+        return per_device(values, points0, points1, points2, tiles_a0, tiles_e1, tiles_a1, factor)
+    c = lax.axis_index("col")
+    D, N2 = nr * nc, nr * R2
+    T0, T1 = R0 // TILE, R1 // TILE
+    B0, B1 = R0 * nr // nc // TILE, R1 * nr // nc // TILE
+    S0 = R0 // nc
+    I0 = S0 // TILE
+    C1, CR, Q1 = B1 * TILE, N2 // D, R1 // nc
+    p0, p1, p2 = (p.astype(jnp.float32) for p in (points0, points1, points2))
+    rows = [p0.reshape(2 * T0, TILE), p1.reshape(2 * T1, TILE),
+            jnp.pad(p2, ((0, 0), (0, TILE - R2))), jnp.pad(p2, ((0, 0), (TILE - R2, 0)))]
+    used = 2 * T0 + 2 * T1 + 4
+    NP = -(-used // 8) * 8
+    pts = jnp.pad(jnp.concatenate(rows, axis=0), ((0, NP - used), (0, 0)))
+    far_a0 = far_of(tiles_a0[0, 0], T0, B0)
+    far_e1 = far_of(tiles_e1[0, 0], T0, B1)
+    far_a1 = far_of(tiles_a1[0, 0], T1, B1)
+    NO = I0 * (B0 + B1)
+    NOP = -(-NO // 8) * 8
+    per_peer = jnp.concatenate([far_a0.reshape(nc, I0 * B0), far_e1.reshape(nc, I0 * B1)], axis=1)
+    per_peer = jnp.pad(per_peer, ((0, 0), (0, NOP - NO)))
+    offs = jnp.broadcast_to(per_peer[:, :, None], (nc, NOP, TILE))
+    offe = jnp.broadcast_to(far_e1.T.reshape(-1, 1), (B1 * T0, TILE))
+    offa = jnp.broadcast_to(far_a1.reshape(-1, 1), (T1 * B1, TILE))
+    width = factor.shape[1]
+    fac = lax.dynamic_update_slice(jnp.zeros((R2, TILE), factor.dtype), factor, (0, lax.rem(c, TILE // width) * width))
+    g = dict(nr=nr, nc=nc, R0=R0, R1=R1, R2=R2, N2=N2,
+             scale_a0=(R0 / (nc * tiles_a0.shape[-1] * TILE * TILE)) ** 0.5,
+             scale_e1=(R0 / (nc * tiles_e1.shape[-1] * TILE * TILE)) ** 0.5,
+             scale_a1=(R1 / (nc * tiles_a1.shape[-1] * TILE * TILE)) ** 0.5,
+             scale_e2=(1.0 / (R1 * nr)) ** 0.5,
+             norm_scale=1.0 / (R0 * nr * F))
+    f32, bf16 = jnp.float32, jnp.bfloat16
+    V = pltpu.VMEM
+    dma = pltpu.SemaphoreType.DMA
+    scratch = [
+        V((nr, NP, TILE), f32), V((nc, NOP, TILE), f32), V((nc, R2, TILE), bf16),
+        V((nr, R0, F), bf16), V((nr, S0, R0), bf16), V((S0, nr * R1), bf16), V((C1, R0), bf16),
+        V((nr * R1, N2), bf16), V((N2, R1 + C1), bf16), V((R1, C1), bf16),
+        V((2 * I0, TILE, TILE), f32), V((nr * T1, 2, TILE, TILE), f32), V((2 * N2 // TILE, TILE, TILE), f32),
+        V((R0, F), bf16), V((nr, Q1, F), f32), V((nr, Q1, F), f32), V((nr, Q1, F), f32),
+        V((nr, nc, Q1, F), bf16), V((R1 + C1, F), bf16), V((D, CR + 8, F), f32), V((D, CR + 8, F), f32),
+        V((N2, F), f32), V((nr, R2, N2), bf16), V((N2, N2), bf16), V((N2, F), f32), V((nr * R1, F), bf16),
+    ]
+    for n in (nr, nc, nc, CHUNKS, CHUNKS, CHUNKS, CHUNKS, 1, nr, nc, nr, nr, nc, nr, D, D):
+        scratch += [dma((n,)), dma((n,))]
+    vm = pl.BlockSpec(memory_space=pltpu.VMEM)
+    fine, mid, coarse, norm = pl.pallas_call(
+        functools.partial(cycle_kernel, g),
+        out_shape=(jax.ShapeDtypeStruct((S0, F), f32), jax.ShapeDtypeStruct((C1, F), f32),
+                   jax.ShapeDtypeStruct((R2, F), f32), jax.ShapeDtypeStruct((8, TILE), f32)),
+        in_specs=[vm] * 6,
+        out_specs=[vm] * 4,
+        scratch_shapes=scratch,
+        compiler_params=pltpu.CompilerParams(collective_id=0, has_side_effects=True, vmem_limit_bytes=48 << 20),
+    )(values, pts, offs, fac, offe, offa)
+    return (fine, mid, coarse, norm[0, :1])
+
+
 def solution(mesh):
     return jax.shard_map(
-        per_device,
+        fused,
         mesh=mesh,
         in_specs=(
             P("row", None),

time: 502 us -> 73.4 us (0.15)
  waiting for transfers between devices: 289 us -> 0 us
  blocking collectives: 129 us -> 0 us
  Pallas kernels: 0 us -> 62.4 us
  local copies, waits for them, and re-layouts: 31.9 us -> 8.96 us
  other arithmetic: 23.1 us -> 0.47 us
  between operations: 16.8 us -> 0.72 us
  matrix products: 10.9 us -> 0 us
    psum x6 -> x0, waiting for transfers between devices: 264 us -> none  [the longest x1 77 us: per_device(): product_whole = lax.psum(product_part, 'col')]
    psum x5 -> x0, blocking collectives: 129 us -> none  [the longest x1 39.4 us: per_device(): fine_total = lax.psum(fine_square / col_count, ('row', 'col'))]
    pallas_call x0 -> x1, Pallas kernels: none -> 62.4 us  [fused(): pl.pallas_call(functools.partial(cycle_kernel, g), out_shape=(jax.ShapeDt...]
    gather x42 -> x0, local copies, waits for them, and re-layouts: 24.4 us -> none  [the longest x28 16.1 us: add_group(): kernel = wendland(row_tiles[:, tile_rows], col_tiles[:, tile_cols], support)]
    reduce_scatter x1 -> x0, waiting for transfers between devices: 24.1 us -> none  [per_device(): lax.psum_scatter(fine_part, 'col', scatter_dimension=0, tiled=True)]
    scatter-add x14 -> x0, other arithmetic: 13.1 us -> none  [the longest x9 9.33 us: add_group(): return (total.at[tile_rows].add(contrib), None)]
    dot_general x18 -> x0, matrix products: 10.9 us -> none  [the longest x9 6.72 us: add_group(): jnp.einsum('gij,gjr->gir', kernel, inputs[tile_cols], preferred_element_t...]
  transfers between devices with their start and end apart: 7 -> 0, of which waited for: 7 -> 0; matrix products, arithmetic and copies ran while one was open for 0% -> 0% of each run, Pallas kernels for 0% -> 0%
where the time goes in v1:
time: 73.4 us; the launch traced here: 72.5 us
  Pallas kernels  62.4 us (85%)
  local copies, waits for them, and re-layouts  8.96 us (12%)
    pallas_call x1, Pallas kernels, fused(): pl.pallas_call(functools.partial(cycle_kernel, g), out_shape=(jax.ShapeDt...  62.4 us
    unnamed x20, local copies, waits for them, and re-layouts  7.64 us

profile of v1, /device:TPU:0, one launch (start us, length us, event | category | flops | bytes accessed | tf_op | source)
XLA Modules:
  0.0 72.5 jit_solution(9142051088886172233)
XLA Ops:
  0.6 0.0 copy-start.4
  0.6 0.7 copy-done.4
  1.3 0.1 fusion
  1.4 0.0 copy-start.5
  1.4 0.7 copy-done.5
  2.1 0.1 fusion.2
  2.2 0.0 copy-start.6
  2.2 0.7 copy-done.6
  2.9 0.1 fusion.3
  3.0 0.0 copy-start.7
  3.0 0.6 copy-done.7
  3.6 0.1 broadcast_in_dim.61.offa
  3.7 0.1 select_n.32
  3.8 0.1 select_n.34
  3.9 0.0 copy-start.3
  3.9 0.1 select_maximum_fusion.2
  3.9 0.6 copy-done.3
  4.6 0.1 select_n.36
  4.6 0.1 copy.17
  4.7 0.1 broadcast_in_dim.57
  4.8 0.0 copy-start.1
  4.8 0.1 broadcast_in_dim.58.offe
  4.9 0.6 copy-done.1
  5.5 0.1 select_maximum_fusion
  5.6 0.0 copy-start.2
  5.6 0.7 copy-done.2
  6.3 0.1 copy.16
  6.4 0.2 dynamic_update_slice.3.fac
  6.6 0.1 broadcast_in_dim.55.offs
  6.7 0.0 copy-start
  6.7 1.0 %copy-done = bf16[2048,128]{1,0:T(8,128)(2,1)S(1)} copy-done((bf16[2048,128]{1,0:T(8,128)(2,1)S(1)}, bf16[2048,128]{1,0:T(8,128)(2,1)}, u32[]{:S(2)}) %copy-start) | copy-done | bytes 524312
  7.7 62.4 %shard_map.111 = (f32[256,128]{1,0:T(8,128)S(1)}, f32[256,128]{1,0:T(8,128)S(1)}, f32[64,128]{1,0:T(8,128)S(1)}, f32[8,128]{1,0:T(8,128)S(1)}) custom-call(bf16[2048,128]{1,0:T(8,128)(2,1)S(1)} %copy-done, f32[48,128]{1,0:T(8,128)S(1)} %pad.18.pts, f32[8,24,128]{2,1,0:T(8,128)S(1)} %broadcast_in_dim.55.offs, bf16[64,128]{1,0:T(8,128)(2,1)S(1)} %dynamic_update_slice.3.fac, ...), custom_call_target="tpu_custom_call" | custom-call | tf_op jit(solution)/shard_map/pallas_call | solution.py:510
  70.1 0.5 slice.33
  70.6 0.7 copy.22
  71.3 0.7 copy.23
  71.9 0.6 copy.24
  (11 shorter events, 0.1 us)
Async XLA Ops:
  0.6 0.7 copy-start.4
  1.4 0.7 copy-start.5
  2.2 0.7 copy-start.6
  3.0 0.7 copy-start.7
  3.9 0.7 copy-start.3
  4.8 0.7 copy-start.1
  5.6 0.7 copy-start.2
  6.7 1.0 %copy-start = (bf16[2048,128]{1,0:T(8,128)(2,1)S(1)}, bf16[2048,128]{1,0:T(8,128)(2,1)}, u32[]{:S(2)}) copy-start(bf16[2048,128]{1,0:T(8,128)(2,1)} %vals.1) | copy-start | bytes 1572868

commit v2 on v1

--- a/solution.py
+++ b/solution.py
@@ -151,8 +151,17 @@
     return jnp.dot(a, b, preferred_element_type=jnp.float32)
 
 
-def cycle_kernel(g, vals, pts, offs, fac, offe, offa, fine_o, mid_o, coarse_o, norm_o,
-                 ptsg, offg, facg, vall, a0, e1own, e1t, e2t, e2c, a1, cf, cm, cc2, resg, part_buf,
+def far_rows(tiles, row_tiles, col_tiles, by_col):
+    row, col = tiles[0, 0, 0:1, :], tiles[0, 0, 1:2, :]
+    key = col * row_tiles + row if by_col else row * col_tiles + col
+    count = row_tiles * col_tiles
+    place = lax.broadcasted_iota(jnp.int32, (count, key.shape[1]), 0)
+    near = jnp.max(jnp.where(place == key, 1.0, 0.0), axis=1, keepdims=True)
+    return jnp.broadcast_to(FAR * (1.0 - near), (count, TILE))
+
+
+def cycle_kernel(g, vals, points0, points1, points2, tiles_a0, tiles_e1, tiles_a1, factor, fine_o, mid_o, coarse_o, norm_o,
+                 pts, offs, fac, offe, offa, ptsg, offg, facg, vall, a0, e1own, e1t, e2t, e2c, a1, cf, cm, cc2, resg, part_buf,
                  rsin, midc, mida, rhs, csend, crecv, cg, gall, gt, ccoef, mcb,
                  p_s, p_r, o_s, o_r, f_s, f_r, vy_s, vy_r, vx_s, vx_r, vf_s, vf_r, vg_s, vg_r, vp_s, vp_r,
                  g_s, g_r, res_s, res_r, rs_s, rs_r, mc_s, mc_r, mq_s, mq_r, mf_s, mf_r, cr_s, cr_r, ca_s, ca_r):
@@ -197,6 +206,17 @@
     each(1, D, greet)
     pl.semaphore_wait(barrier, D - 1)
 
+    pts[...] = jnp.zeros_like(pts)
+    for way in range(2):
+        for ref, at, count in ((points0, way * T0, T0), (points1, X1 + way * T1, T1)):
+            line = ref[way:way + 1, :].astype(jnp.float32)
+            for k in range(count):
+                pts[at + k:at + k + 1, :] = line[:, k * TILE:(k + 1) * TILE]
+        line = points2[way:way + 1, :].astype(jnp.float32)
+        blank = jnp.zeros((1, TILE - R2), jnp.float32)
+        pts[X2 + way:X2 + way + 1, :] = jnp.concatenate([line, blank], axis=1)
+        pts[X2 + 2 + way:X2 + 3 + way, :] = jnp.concatenate([blank, line], axis=1)
+
     def row_send(src_of, dst, ss, rr):
         for k in range(1, nr):
             q = lax.rem(r + k, nr)
@@ -219,6 +239,16 @@
             rc(src, dst_of(q), ss.at[k], rr.at[q], r, q).wait()
         each(1, nc, go)
 
+    far_a0 = far_rows(tiles_a0, T0, B0, False)
+    far_e1 = far_rows(tiles_e1, T0, B1, False)
+    offs[...] = jnp.zeros_like(offs)
+    for q in range(nc):
+        offs[q, :I0 * B0] = far_a0[q * I0 * B0:(q + 1) * I0 * B0]
+        offs[q, I0 * B0:I0 * (B0 + B1)] = far_e1[q * I0 * B1:(q + 1) * I0 * B1]
+    wide = factor.shape[1]
+    lane_of = lax.rem(c, TILE // wide)
+    raw = factor[...].astype(jnp.float32)
+    fac[...] = jnp.concatenate([jnp.where(lane_of == k, raw, 0.0) for k in range(TILE // wide)], axis=1).astype(jnp.bfloat16)
     row_send(lambda q: pts, ptsg.at[r], p_s, p_r)
     HALF = R0 // 2
     CH = HALF // CHUNKS
@@ -259,6 +289,9 @@
     ptsg[r] = pts[...]
     offg[c] = offs[c]
     facg[c] = fac[...]
+
+    offe[...] = far_rows(tiles_e1, T0, B1, True)
+    offa[...] = far_rows(tiles_a1, T1, B1, False)
 
     def turned(row):
         return jnp.broadcast_to(row, (TILE, TILE)).T
@@ -298,18 +331,27 @@
     acc = acc + dot(a0[3], vall[diag])
     own_vals = vals[pl.ds(pl.multiple_of(c * S0, S0), S0), :].astype(jnp.float32)
     res = own_vals - (0.5 * g["scale_a0"]) * acc
-    square = jnp.sum((res * res).reshape(S0 // 8, 8, -1), axis=0)
 
     def res_at(q):
         return resg.at[pl.ds(pl.multiple_of(q * S0, S0), S0)]
 
     resg[pl.ds(pl.multiple_of(c * S0, S0), S0), :] = res.astype(jnp.bfloat16)
-    col_send(lambda q: res_at(c), res_at(c), res_s, res_r)
+    for k in range(1, nc // 2):
+        q = lax.rem(c + 2 * k, nc)
+        rc(res_at(c), res_at(c), res_s.at[k], res_r.at[c], r, q).start()
+    rc(res_at(c), res_at(c), res_s.at[0], res_r.at[c], r, xp).start()
+
+    def res_pass(k):
+        q = lax.rem(c + 2 * k, nc)
+        rc(res_at(c), res_at(q), res_s.at[k], res_r.at[q], r, q).wait_recv()
+        rc(res_at(q), res_at(q), res_s.at[nc // 2 + k], res_r.at[q], r, xp).start()
+
 
     def turn_mid(k):
         for way in range(2):
             cm[k, way] = turned(ptsg[k // T1, pl.ds(X1 + way * T1 + lax.rem(k, T1), 1), :])
     each(0, NT1, turn_mid)
+    res_pass(1)
 
     def build_e1t(i):
         rx, ry = pts[pl.ds(i, 1), :], pts[pl.ds(T0 + i, 1), :]
@@ -318,6 +360,9 @@
             e1t[j * TILE:(j + 1) * TILE, pl.ds(pl.multiple_of(i * TILE, TILE), TILE)] = phi_tile(
                 cm[c * B1 + j, 0], cm[c * B1 + j, 1], rx + off, ry, mid_inv)
     each(0, T0, build_e1t)
+    res_pass(nc // 2 - 1)
+    for k in range(2, nc // 2 - 1):
+        res_pass(k)
     col_wait(fac, lambda q: facg.at[q], f_s, f_r)
     per_lane = nc * TILE // g["N2"]
     for lane in range(g["N2"] // TILE):
@@ -352,6 +397,41 @@
                 cc2[2 * t], cc2[2 * t + 1], rx, ry, coarse_inv)
     each(0, T1 + B1, build_e2c)
 
+    for k in range(1, nc // 2):
+        q = lax.rem(c + 2 * k, nc)
+        rc(res_at(c), res_at(c), res_s.at[k], res_r.at[c], r, q).wait_send()
+        rc(res_at(q), res_at(q), res_s.at[nc // 2 + k], res_r.at[q], r, xp).wait_send()
+        qx = lax.rem(xp + 2 * k, nc)
+        rc(res_at(qx), res_at(qx), res_s.at[0], res_r.at[qx], r, xp).wait_recv()
+    rc(res_at(c), res_at(c), res_s.at[0], res_r.at[c], r, xp).wait_send()
+    rc(res_at(c), res_at(xp), res_s.at[0], res_r.at[xp], r, xp).wait_recv()
+    held = resg[...].astype(jnp.float32)
+    square = jnp.sum((held * held).reshape(R0 // 8, 8, -1), axis=0)
+    part_buf[...] = dot(e1t[...], resg[...]).reshape(nr, Q1, -1)
+    row_send(lambda q: part_buf.at[q], rsin.at[r], rs_s, rs_r)
+    rsin[r] = part_buf[r]
+    row_wait(part_buf.at[0], lambda q: rsin.at[q], rs_s, rs_r)
+    quarter = rsin[0]
+    for k in range(1, nr):
+        quarter = quarter + rsin[k]
+    quarter = g["scale_e1"] * quarter
+    midc[r] = jnp.concatenate([quarter, square], axis=0)
+    mida[r, c] = quarter.astype(jnp.bfloat16)
+    row_send(lambda q: midc.at[r], midc.at[r], mc_s, mc_r)
+    col_send(lambda q: mida.at[r, c], mida.at[r, c], mq_s, mq_r)
+    row_wait(midc.at[r], lambda q: midc.at[q], mc_s, mc_r)
+    mid_f32 = midc[:, :Q1].reshape(C1, -1)
+    mid_col = mid_f32.astype(jnp.bfloat16)
+    rhs[:R1] = ((-0.5 * g["scale_a1"]) * dot(a1[...], mid_col)).astype(jnp.bfloat16)
+    for k in range(nr):
+        rhs[R1 + k * Q1:R1 + (k + 1) * Q1] = jnp.where(r == k, midc[k, :Q1], 0.0).astype(jnp.bfloat16)
+    csend[...] = (g["scale_e2"] * dot(e2c[...], rhs[...])).reshape(D, CR, -1)
+
+    def cr_go(k):
+        peer = lax.rem(d + k, D)
+        rc(csend.at[peer], crecv.at[d], cr_s.at[k], cr_r.at[d], peer // nc, lax.rem(peer, nc)).start()
+    each(1, D, cr_go)
+    crecv[d] = csend[d]
     def build_e1own(k):
         rx = ptsg[k // T1, pl.ds(X1 + lax.rem(k, T1), 1), :]
         ry = ptsg[k // T1, pl.ds(Y1 + lax.rem(k, T1), 1), :]
@@ -369,33 +449,6 @@
     row_wait(gall.at[r], lambda q: gall.at[q], g_s, g_r)
     whole = gall[...].reshape(g["N2"], g["N2"])
     gt[...] = whole.astype(jnp.float32).T.astype(jnp.bfloat16)
-
-    col_wait(res_at(c), res_at, res_s, res_r)
-    part_buf[...] = dot(e1t[...], resg[...]).reshape(nr, Q1, -1)
-    row_send(lambda q: part_buf.at[q], rsin.at[r], rs_s, rs_r)
-    rsin[r] = part_buf[r]
-    row_wait(part_buf.at[0], lambda q: rsin.at[q], rs_s, rs_r)
-    quarter = rsin[0]
-    for k in range(1, nr):
-        quarter = quarter + rsin[k]
-    quarter = g["scale_e1"] * quarter
-    midc[r] = quarter
-    mida[r, c] = quarter.astype(jnp.bfloat16)
-    row_send(lambda q: midc.at[r], midc.at[r], mc_s, mc_r)
-    col_send(lambda q: mida.at[r, c], mida.at[r, c], mq_s, mq_r)
-    row_wait(midc.at[r], lambda q: midc.at[q], mc_s, mc_r)
-    mid_col = midc[...].reshape(C1, -1).astype(jnp.bfloat16)
-    rhs[:R1] = ((-0.5 * g["scale_a1"]) * dot(a1[...], mid_col)).astype(jnp.bfloat16)
-    for k in range(nr):
-        rhs[R1 + k * Q1:R1 + (k + 1) * Q1] = jnp.where(r == k, midc[k], 0.0).astype(jnp.bfloat16)
-    csend[:, :CR] = (g["scale_e2"] * dot(e2c[...], rhs[...])).reshape(D, CR, -1)
-    csend[:, CR:] = jnp.broadcast_to(square[None], (D,) + square.shape)
-
-    def cr_go(k):
-        peer = lax.rem(d + k, D)
-        rc(csend.at[peer], crecv.at[d], cr_s.at[k], cr_r.at[d], peer // nc, lax.rem(peer, nc)).start()
-    each(1, D, cr_go)
-    crecv[d] = csend[d]
     col_wait(mida.at[r, c], lambda q: mida.at[r, q], mq_s, mq_r)
     def cr_wait(k):
         peer = lax.rem(d + k, D)
@@ -406,14 +459,14 @@
     def cg_at(q):
         return cg.at[pl.ds(pl.multiple_of(q * CR, CR), CR)]
 
-    cg[pl.ds(pl.multiple_of(d * CR, CR), CR), :] = sums[:CR]
+    cg[pl.ds(pl.multiple_of(d * CR, CR), CR), :] = sums
 
     def ca_go(k):
         peer = lax.rem(d + k, D)
         rc(cg_at(d), cg_at(d), ca_s.at[k], ca_r.at[d], peer // nc, lax.rem(peer, nc)).start()
     each(1, D, ca_go)
     row_send(lambda q: mida.at[r], mida.at[r], mf_s, mf_r)
-    norm_o[...] = jnp.broadcast_to(jnp.sum(sums[CR:], keepdims=True) * g["norm_scale"], norm_o.shape)
+    norm_o[...] = jnp.broadcast_to(jnp.sum(jnp.sum(midc[:, Q1:], axis=0), keepdims=True) * g["norm_scale"], norm_o.shape)
     def ca_wait(k):
         peer = lax.rem(d + k, D)
         rc(cg_at(d), cg_at(peer), ca_s.at[k], ca_r.at[peer], peer // nc, lax.rem(peer, nc)).wait()
@@ -423,7 +476,7 @@
     coarse_o[...] = ccoef[pl.ds(pl.multiple_of(r * R2, R2), R2), :]
     coarse_low = ccoef[...].astype(jnp.bfloat16)
     own_rows = pl.ds(pl.multiple_of(c * C1, C1), C1)
-    mid_o[...] = 0.5 * midc[...].reshape(C1, -1) + g["scale_e2"] * dot(e2t[own_rows, :], coarse_low)
+    mid_o[...] = 0.5 * midc[:, :Q1].reshape(C1, -1) + g["scale_e2"] * dot(e2t[own_rows, :], coarse_low)
     row_wait(mida.at[r], lambda q: mida.at[q], mf_s, mf_r)
     for q in range(nc):
         corr = g["scale_e2"] * dot(e2t[q * C1:(q + 1) * C1, :], coarse_low)
@@ -439,12 +492,6 @@
     mate_copy.wait_send()
 
 
-def far_of(listing, row_tiles, col_tiles):
-    key = listing[0] * col_tiles + listing[1]
-    hit = jnp.any(jnp.arange(row_tiles * col_tiles)[:, None] == key[None, :], axis=1)
-    return jnp.where(hit, 0.0, FAR).astype(jnp.float32).reshape(row_tiles, col_tiles)
-
-
 def fits(nr, nc, R0, R1, R2):
     if nr != 4 or nc % nr or (nc // nr) % 2:
         return False
@@ -461,31 +508,16 @@
     F = values.shape[-1]
     if not fits(nr, nc, R0, R1, R2) or F != TILE:
         return per_device(values, points0, points1, points2, tiles_a0, tiles_e1, tiles_a1, factor)
-    c = lax.axis_index("col")
     D, N2 = nr * nc, nr * R2
     T0, T1 = R0 // TILE, R1 // TILE
     B0, B1 = R0 * nr // nc // TILE, R1 * nr // nc // TILE
     S0 = R0 // nc
     I0 = S0 // TILE
     C1, CR, Q1 = B1 * TILE, N2 // D, R1 // nc
-    p0, p1, p2 = (p.astype(jnp.float32) for p in (points0, points1, points2))
-    rows = [p0.reshape(2 * T0, TILE), p1.reshape(2 * T1, TILE),
-            jnp.pad(p2, ((0, 0), (0, TILE - R2))), jnp.pad(p2, ((0, 0), (TILE - R2, 0)))]
     used = 2 * T0 + 2 * T1 + 4
     NP = -(-used // 8) * 8
-    pts = jnp.pad(jnp.concatenate(rows, axis=0), ((0, NP - used), (0, 0)))
-    far_a0 = far_of(tiles_a0[0, 0], T0, B0)
-    far_e1 = far_of(tiles_e1[0, 0], T0, B1)
-    far_a1 = far_of(tiles_a1[0, 0], T1, B1)
     NO = I0 * (B0 + B1)
     NOP = -(-NO // 8) * 8
-    per_peer = jnp.concatenate([far_a0.reshape(nc, I0 * B0), far_e1.reshape(nc, I0 * B1)], axis=1)
-    per_peer = jnp.pad(per_peer, ((0, 0), (0, NOP - NO)))
-    offs = jnp.broadcast_to(per_peer[:, :, None], (nc, NOP, TILE))
-    offe = jnp.broadcast_to(far_e1.T.reshape(-1, 1), (B1 * T0, TILE))
-    offa = jnp.broadcast_to(far_a1.reshape(-1, 1), (T1 * B1, TILE))
-    width = factor.shape[1]
-    fac = lax.dynamic_update_slice(jnp.zeros((R2, TILE), factor.dtype), factor, (0, lax.rem(c, TILE // width) * width))
     g = dict(nr=nr, nc=nc, R0=R0, R1=R1, R2=R2, N2=N2,
              scale_a0=(R0 / (nc * tiles_a0.shape[-1] * TILE * TILE)) ** 0.5,
              scale_e1=(R0 / (nc * tiles_e1.shape[-1] * TILE * TILE)) ** 0.5,
@@ -496,12 +528,13 @@
     V = pltpu.VMEM
     dma = pltpu.SemaphoreType.DMA
     scratch = [
+        V((NP, TILE), f32), V((nc, NOP, TILE), f32), V((R2, TILE), bf16), V((B1 * T0, TILE), f32), V((T1 * B1, TILE), f32),
         V((nr, NP, TILE), f32), V((nc, NOP, TILE), f32), V((nc, R2, TILE), bf16),
         V((nr, R0, F), bf16), V((nr, S0, R0), bf16), V((S0, nr * R1), bf16), V((C1, R0), bf16),
         V((nr * R1, N2), bf16), V((N2, R1 + C1), bf16), V((R1, C1), bf16),
         V((2 * I0, TILE, TILE), f32), V((nr * T1, 2, TILE, TILE), f32), V((2 * N2 // TILE, TILE, TILE), f32),
-        V((R0, F), bf16), V((nr, Q1, F), f32), V((nr, Q1, F), f32), V((nr, Q1, F), f32),
-        V((nr, nc, Q1, F), bf16), V((R1 + C1, F), bf16), V((D, CR + 8, F), f32), V((D, CR + 8, F), f32),
+        V((R0, F), bf16), V((nr, Q1, F), f32), V((nr, Q1, F), f32), V((nr, Q1 + 8, F), f32),
+        V((nr, nc, Q1, F), bf16), V((R1 + C1, F), bf16), V((D, CR, F), f32), V((D, CR, F), f32),
         V((N2, F), f32), V((nr, R2, N2), bf16), V((N2, N2), bf16), V((N2, F), f32), V((nr * R1, F), bf16),
     ]
     for n in (nr, nc, nc, CHUNKS, CHUNKS, CHUNKS, CHUNKS, 1, nr, nc, nr, nr, nc, nr, D, D):
@@ -511,11 +544,11 @@
         functools.partial(cycle_kernel, g),
         out_shape=(jax.ShapeDtypeStruct((S0, F), f32), jax.ShapeDtypeStruct((C1, F), f32),
                    jax.ShapeDtypeStruct((R2, F), f32), jax.ShapeDtypeStruct((8, TILE), f32)),
-        in_specs=[vm] * 6,
+        in_specs=[vm] * 8,
         out_specs=[vm] * 4,
         scratch_shapes=scratch,
         compiler_params=pltpu.CompilerParams(collective_id=0, has_side_effects=True, vmem_limit_bytes=48 << 20),
-    )(values, pts, offs, fac, offe, offa)
+    )(values, points0, points1, points2, tiles_a0, tiles_e1, tiles_a1, factor)
     return (fine, mid, coarse, norm[0, :1])
 
 

time: 73.4 us -> 65.3 us (0.89)
  local copies, waits for them, and re-layouts: 8.96 us -> 4.32 us
  Pallas kernels: 62.4 us -> 59.6 us
    unnamed x20 -> x18, local copies, waits for them, and re-layouts: 7.64 us -> 3.81 us
    pallas_call x1, Pallas kernels: 62.4 us -> 59.6 us  [fused(): pl.pallas_call(functools.partial(cycle_kernel, g), out_shape=(jax.ShapeDt...]
where the time goes in v2:
time: 65.3 us; the launch traced here: 64.7 us
  Pallas kernels  59.6 us (91%)
  local copies, waits for them, and re-layouts  4.32 us (7%)
  between operations  0.74 us (1%)
    pallas_call x1, Pallas kernels, fused(): pl.pallas_call(functools.partial(cycle_kernel, g), out_shape=(jax.ShapeDt...  59.6 us
    unnamed x18, local copies, waits for them, and re-layouts  3.81 us

profile of v2, /device:TPU:0, one launch (start us, length us, event | category | flops | bytes accessed | tf_op | source)
XLA Modules:
  0.0 64.7 jit_solution(6712603175108822426)
XLA Ops:
  0.6 0.0 copy-start.5
  0.6 0.0 copy-start.4
  0.7 0.0 copy-start.3
  0.7 0.0 copy-start.6
  0.7 0.0 copy-start.2
  0.7 0.0 copy-start.1
  0.7 0.8 %copy.12.factor = bf16[64,32]{1,0:T(8,128)(2,1)S(1)} copy(bf16[64,32]{0,1:T(8,128)(2,1)} %param.15) | data formatting | bytes 8192 | tf_op args[7]
  1.5 0.0 copy-done.5
  1.5 0.0 copy-done.4
  1.5 0.0 copy-done.3
  1.5 0.0 copy-done.6
  1.6 0.0 copy-done.2
  1.6 0.0 copy-done.1
  1.6 0.0 copy-start
  1.6 1.0 %copy-done = bf16[2048,128]{1,0:T(8,128)(2,1)S(1)} copy-done((bf16[2048,128]{1,0:T(8,128)(2,1)S(1)}, bf16[2048,128]{1,0:T(8,128)(2,1)}, u32[]{:S(2)}) %copy-start) | copy-done | bytes 524312
  2.6 59.6 %shard_map.111 = (f32[256,128]{1,0:T(8,128)S(1)}, f32[256,128]{1,0:T(8,128)S(1)}, f32[64,128]{1,0:T(8,128)S(1)}, f32[8,128]{1,0:T(8,128)S(1)}) custom-call(bf16[2048,128]{1,0:T(8,128)(2,1)S(1)} %copy-done, bf16[2,2048]{1,0:T(2,128)(2,1)S(1)} %copy-done.1, bf16[2,512]{1,0:T(2,128)(2,1)S(1)} %copy-done.2, bf16[2,64]{1,0:T(2,128)(2,1)S(1)} %copy-done.6, ...), custom_call_target="tpu_custom_call" | custom-call | tf_op jit(solution)/shard_map/pallas_call | solution.py:543
  62.3 0.5 slice.3
  62.8 0.7 %copy.16 = f32[256,128]{1,0:T(8,128)} copy(f32[256,128]{1,0:T(8,128)S(1)} %get-tuple-element.16) | data formatting | bytes 262144
  63.4 0.7 %copy.17 = f32[256,128]{1,0:T(8,128)} copy(f32[256,128]{1,0:T(8,128)S(1)} %get-tuple-element.17) | data formatting | bytes 262144
  64.1 0.6 copy.18
Async XLA Ops:
  0.6 0.9 %copy-start.5 = (s32[1,1,2,4]{3,2,1,0:T(2,128)S(1)}, s32[1,1,2,4]{3,2,1,0:T(2,128)}, u32[]{:S(2)}) copy-start(s32[1,1,2,4]{3,2,1,0:T(2,128)} %tiles_a1.1) | copy-start | bytes 100
  0.6 0.9 %copy-start.4 = (s32[1,1,2,20]{3,2,1,0:T(2,128)S(1)}, s32[1,1,2,20]{3,2,1,0:T(2,128)}, u32[]{:S(2)}) copy-start(s32[1,1,2,20]{3,2,1,0:T(2,128)} %tiles_e1.1) | copy-start | bytes 484
  0.7 0.9 %copy-start.3 = (s32[1,1,2,48]{3,2,1,0:T(2,128)S(1)}, s32[1,1,2,48]{3,2,1,0:T(2,128)}, u32[]{:S(2)}) copy-start(s32[1,1,2,48]{3,2,1,0:T(2,128)} %tiles_a0.1) | copy-start | bytes 1156
  0.7 0.9 %copy-start.6 = (bf16[2,64]{1,0:T(2,128)(2,1)S(1)}, bf16[2,64]{1,0:T(2,128)(2,1)}, u32[]{:S(2)}) copy-start(bf16[2,64]{1,0:T(2,128)(2,1)} %points2.1) | copy-start | bytes 772
  0.7 0.9 %copy-start.2 = (bf16[2,512]{1,0:T(2,128)(2,1)S(1)}, bf16[2,512]{1,0:T(2,128)(2,1)}, u32[]{:S(2)}) copy-start(bf16[2,512]{1,0:T(2,128)(2,1)} %points1.1) | copy-start | bytes 6148
  0.7 0.9 %copy-start.1 = (bf16[2,2048]{1,0:T(2,128)(2,1)S(1)}, bf16[2,2048]{1,0:T(2,128)(2,1)}, u32[]{:S(2)}) copy-start(bf16[2,2048]{1,0:T(2,128)(2,1)} %points0.1) | copy-start | bytes 24580
  1.6 1.0 %copy-start = (bf16[2048,128]{1,0:T(8,128)(2,1)S(1)}, bf16[2048,128]{1,0:T(8,128)(2,1)}, u32[]{:S(2)}) copy-start(bf16[2048,128]{1,0:T(8,128)(2,1)} %vals.1) | copy-start | bytes 1572868

commit v3 on v2

--- a/solution.py
+++ b/solution.py
@@ -239,6 +239,41 @@
             rc(src, dst_of(q), ss.at[k], rr.at[q], r, q).wait()
         each(1, nc, go)
 
+    row_send(lambda q: pts, ptsg.at[r], p_s, p_r)
+    HALF = R0 // 2
+    CH = HALF // CHUNKS
+
+    def chunk(half, q):
+        return pl.ds(pl.multiple_of(half * HALF + q * CH, CH), CH)
+
+    def y_copy(q):
+        return rc(vals.at[chunk(h, q)], vall.at[r, chunk(h, q)], vy_s.at[q], vy_r.at[q], yp, c)
+
+    def y_in(q):
+        return rc(vals.at[chunk(h, q)], vall.at[yp, chunk(h, q)], vy_s.at[q], vy_r.at[q], yp, c)
+
+    def x_copy(q):
+        return rc(vall.at[yp, chunk(h, q)], vall.at[yp, chunk(h, q)], vx_s.at[q], vx_r.at[q], r, xp)
+
+    def x_in(q):
+        return rc(vall.at[yp, chunk(h, q)], vall.at[yp, chunk(1 - h, q)], vx_s.at[q], vx_r.at[q], r, xp)
+
+    def f_copy(q):
+        return rc(vall.at[yp, chunk(h, q)], vall.at[yp, chunk(h, q)], vf_s.at[q], vf_r.at[q], mate, c)
+
+    def f_in(q):
+        return rc(vall.at[yp, chunk(h, q)], vall.at[diag, chunk(h, q)], vf_s.at[q], vf_r.at[q], mate, c)
+
+    def g_copy(q):
+        return rc(vall.at[yp, chunk(1 - h, q)], vall.at[yp, chunk(1 - h, q)], vg_s.at[q], vg_r.at[q], mate, c)
+
+    def g_in(q):
+        return rc(vall.at[yp, chunk(1 - h, q)], vall.at[diag, chunk(1 - h, q)], vg_s.at[q], vg_r.at[q], mate, c)
+
+    for q in range(CHUNKS):
+        y_copy(q).start()
+    mate_copy = rc(vals, vall.at[r], vp_s.at[0], vp_r.at[0], mate, c)
+    mate_copy.start()
     far_a0 = far_rows(tiles_a0, T0, B0, False)
     far_e1 = far_rows(tiles_e1, T0, B1, False)
     offs[...] = jnp.zeros_like(offs)
@@ -249,42 +284,7 @@
     lane_of = lax.rem(c, TILE // wide)
     raw = factor[...].astype(jnp.float32)
     fac[...] = jnp.concatenate([jnp.where(lane_of == k, raw, 0.0) for k in range(TILE // wide)], axis=1).astype(jnp.bfloat16)
-    row_send(lambda q: pts, ptsg.at[r], p_s, p_r)
-    HALF = R0 // 2
-    CH = HALF // CHUNKS
-
-    def chunk(half, q):
-        return pl.ds(pl.multiple_of(half * HALF + q * CH, CH), CH)
-
-    def y_copy(q):
-        return rc(vals.at[chunk(h, q)], vall.at[r, chunk(h, q)], vy_s.at[q], vy_r.at[q], yp, c)
-
-    def y_in(q):
-        return rc(vals.at[chunk(h, q)], vall.at[yp, chunk(h, q)], vy_s.at[q], vy_r.at[q], yp, c)
-
-    def x_copy(q):
-        return rc(vall.at[yp, chunk(h, q)], vall.at[yp, chunk(h, q)], vx_s.at[q], vx_r.at[q], r, xp)
-
-    def x_in(q):
-        return rc(vall.at[yp, chunk(h, q)], vall.at[yp, chunk(1 - h, q)], vx_s.at[q], vx_r.at[q], r, xp)
-
-    def f_copy(q):
-        return rc(vall.at[yp, chunk(h, q)], vall.at[yp, chunk(h, q)], vf_s.at[q], vf_r.at[q], mate, c)
-
-    def f_in(q):
-        return rc(vall.at[yp, chunk(h, q)], vall.at[diag, chunk(h, q)], vf_s.at[q], vf_r.at[q], mate, c)
-
-    def g_copy(q):
-        return rc(vall.at[yp, chunk(1 - h, q)], vall.at[yp, chunk(1 - h, q)], vg_s.at[q], vg_r.at[q], mate, c)
-
-    def g_in(q):
-        return rc(vall.at[yp, chunk(1 - h, q)], vall.at[diag, chunk(1 - h, q)], vg_s.at[q], vg_r.at[q], mate, c)
-
-    for q in range(CHUNKS):
-        y_copy(q).start()
     col_send(lambda q: offs.at[q], offg.at[c], o_s, o_r)
-    mate_copy = rc(vals, vall.at[r], vp_s.at[0], vp_r.at[0], mate, c)
-    mate_copy.start()
     col_send(lambda q: fac, facg.at[c], f_s, f_r)
     ptsg[r] = pts[...]
     offg[c] = offs[c]
@@ -465,19 +465,28 @@
         peer = lax.rem(d + k, D)
         rc(cg_at(d), cg_at(d), ca_s.at[k], ca_r.at[d], peer // nc, lax.rem(peer, nc)).start()
     each(1, D, ca_go)
-    row_send(lambda q: mida.at[r], mida.at[r], mf_s, mf_r)
+    mate_slab = rc(mida.at[r], mida.at[r], mf_s.at[0], mf_r.at[r], mate, c)
+    pair_slab = rc(mida.at[r], mida.at[r], mf_s.at[1], mf_r.at[r], yp, c)
+    pair_slab.start()
+    mate_slab.start()
     norm_o[...] = jnp.broadcast_to(jnp.sum(jnp.sum(midc[:, Q1:], axis=0), keepdims=True) * g["norm_scale"], norm_o.shape)
     def ca_wait(k):
         peer = lax.rem(d + k, D)
         rc(cg_at(d), cg_at(peer), ca_s.at[k], ca_r.at[peer], peer // nc, lax.rem(peer, nc)).wait()
     each(1, D, ca_wait)
+    rc(mida.at[r], mida.at[yp], mf_s.at[1], mf_r.at[yp], yp, c).wait_recv()
+    passed_slab = rc(mida.at[yp], mida.at[yp], mf_s.at[2], mf_r.at[yp], mate, c)
+    passed_slab.start()
     halfway = dot(gt[...], cg[...].astype(jnp.bfloat16)).astype(jnp.bfloat16)
     ccoef[...] = dot(gall[...].reshape(g["N2"], g["N2"]), halfway)
     coarse_o[...] = ccoef[pl.ds(pl.multiple_of(r * R2, R2), R2), :]
     coarse_low = ccoef[...].astype(jnp.bfloat16)
     own_rows = pl.ds(pl.multiple_of(c * C1, C1), C1)
     mid_o[...] = 0.5 * midc[:, :Q1].reshape(C1, -1) + g["scale_e2"] * dot(e2t[own_rows, :], coarse_low)
-    row_wait(mida.at[r], lambda q: mida.at[q], mf_s, mf_r)
+    rc(mida.at[r], mida.at[mate], mf_s.at[0], mf_r.at[mate], mate, c).wait_recv()
+    rc(mida.at[yp], mida.at[diag], mf_s.at[2], mf_r.at[diag], mate, c).wait_recv()
+    for slab in (mate_slab, pair_slab, passed_slab):
+        slab.wait_send()
     for q in range(nc):
         corr = g["scale_e2"] * dot(e2t[q * C1:(q + 1) * C1, :], coarse_low)
         for k in range(nr):

time: 65.3 us -> 64.2 us (0.983)
    pallas_call x1, Pallas kernels: 59.6 us -> 59 us  [fused(): pl.pallas_call(functools.partial(cycle_kernel, g), out_shape=(jax.ShapeDt...]
where the time goes in v3:
time: 64.2 us; the launch traced here: 64 us
  Pallas kernels  59 us (92%)
  local copies, waits for them, and re-layouts  4.32 us (7%)
  between operations  0.74 us (1%)
    pallas_call x1, Pallas kernels, fused(): pl.pallas_call(functools.partial(cycle_kernel, g), out_shape=(jax.ShapeDt...  59 us
    unnamed x18, local copies, waits for them, and re-layouts  3.81 us

profile of v3, /device:TPU:0, one launch (start us, length us, event | category | flops | bytes accessed | tf_op | source)
XLA Modules:
  0.0 64.0 jit_solution(3294326875388873243)
XLA Ops:
  0.6 0.0 copy-start.5
  0.6 0.0 copy-start.4
  0.7 0.0 copy-start.3
  0.7 0.0 copy-start.6
  0.7 0.0 copy-start.2
  0.7 0.0 copy-start.1
  0.7 0.8 %copy.12.factor = bf16[64,32]{1,0:T(8,128)(2,1)S(1)} copy(bf16[64,32]{0,1:T(8,128)(2,1)} %param.15) | data formatting | bytes 8192 | tf_op args[7]
  1.5 0.0 copy-done.5
  1.5 0.0 copy-done.4
  1.5 0.0 copy-done.3
  1.5 0.0 copy-done.6
  1.6 0.0 copy-done.2
  1.6 0.0 copy-done.1
  1.6 0.0 copy-start
  1.6 1.0 %copy-done = bf16[2048,128]{1,0:T(8,128)(2,1)S(1)} copy-done((bf16[2048,128]{1,0:T(8,128)(2,1)S(1)}, bf16[2048,128]{1,0:T(8,128)(2,1)}, u32[]{:S(2)}) %copy-start) | copy-done | bytes 524312
  2.6 59.0 %shard_map.111 = (f32[256,128]{1,0:T(8,128)S(1)}, f32[256,128]{1,0:T(8,128)S(1)}, f32[64,128]{1,0:T(8,128)S(1)}, f32[8,128]{1,0:T(8,128)S(1)}) custom-call(bf16[2048,128]{1,0:T(8,128)(2,1)S(1)} %copy-done, bf16[2,2048]{1,0:T(2,128)(2,1)S(1)} %copy-done.1, bf16[2,512]{1,0:T(2,128)(2,1)S(1)} %copy-done.2, bf16[2,64]{1,0:T(2,128)(2,1)S(1)} %copy-done.6, ...), custom_call_target="tpu_custom_call" | custom-call | tf_op jit(solution)/shard_map/pallas_call | solution.py:552
  61.6 0.5 slice.3
  62.1 0.7 %copy.16 = f32[256,128]{1,0:T(8,128)} copy(f32[256,128]{1,0:T(8,128)S(1)} %get-tuple-element.16) | data formatting | bytes 262144
  62.8 0.7 %copy.17 = f32[256,128]{1,0:T(8,128)} copy(f32[256,128]{1,0:T(8,128)S(1)} %get-tuple-element.17) | data formatting | bytes 262144
  63.4 0.6 copy.18
Async XLA Ops:
  0.6 0.9 %copy-start.5 = (s32[1,1,2,4]{3,2,1,0:T(2,128)S(1)}, s32[1,1,2,4]{3,2,1,0:T(2,128)}, u32[]{:S(2)}) copy-start(s32[1,1,2,4]{3,2,1,0:T(2,128)} %tiles_a1.1) | copy-start | bytes 100
  0.6 0.9 %copy-start.4 = (s32[1,1,2,20]{3,2,1,0:T(2,128)S(1)}, s32[1,1,2,20]{3,2,1,0:T(2,128)}, u32[]{:S(2)}) copy-start(s32[1,1,2,20]{3,2,1,0:T(2,128)} %tiles_e1.1) | copy-start | bytes 484
  0.7 0.9 %copy-start.3 = (s32[1,1,2,48]{3,2,1,0:T(2,128)S(1)}, s32[1,1,2,48]{3,2,1,0:T(2,128)}, u32[]{:S(2)}) copy-start(s32[1,1,2,48]{3,2,1,0:T(2,128)} %tiles_a0.1) | copy-start | bytes 1156
  0.7 0.9 %copy-start.6 = (bf16[2,64]{1,0:T(2,128)(2,1)S(1)}, bf16[2,64]{1,0:T(2,128)(2,1)}, u32[]{:S(2)}) copy-start(bf16[2,64]{1,0:T(2,128)(2,1)} %points2.1) | copy-start | bytes 772
  0.7 0.9 %copy-start.2 = (bf16[2,512]{1,0:T(2,128)(2,1)S(1)}, bf16[2,512]{1,0:T(2,128)(2,1)}, u32[]{:S(2)}) copy-start(bf16[2,512]{1,0:T(2,128)(2,1)} %points1.1) | copy-start | bytes 6148
  0.7 0.9 %copy-start.1 = (bf16[2,2048]{1,0:T(2,128)(2,1)S(1)}, bf16[2,2048]{1,0:T(2,128)(2,1)}, u32[]{:S(2)}) copy-start(bf16[2,2048]{1,0:T(2,128)(2,1)} %points0.1) | copy-start | bytes 24580
  1.6 1.0 %copy-start = (bf16[2048,128]{1,0:T(8,128)(2,1)S(1)}, bf16[2048,128]{1,0:T(8,128)(2,1)}, u32[]{:S(2)}) copy-start(bf16[2048,128]{1,0:T(8,128)(2,1)} %vals.1) | copy-start | bytes 1572868
